TPU v7x, 768 devices: a whole 4x8x12 slice. The times are simulated.
768 devices in a mesh: rep: 192 (over y, x, z_lo), sp: 4 (over z_hi, core).
Axes of the slice: x: 4, y: 8, z: 12 (z_hi: 2, z_lo: 6; z = z_hi * 6 + z_lo), core: 2. Of those that a mesh axis runs over, the one named last changes fastest.
Arguments:
- field: bfloat16 [192, 128, 100, 128], P('rep', 'sp'), may hold values from -6 to 6
- send_blocks: int32 [4, 4, 8], P('sp'), may hold values from 0 to 31
- send_count: int32 [4, 4], P('sp'), may hold values from 1 to 8, as said below
- regrid_weights: bfloat16 [32, 8, 128, 128], P('sp'), may hold values from -0.1875 to 0.1875
- tile_slot: int32 [32, 8], P('sp'), may hold values from 0 to 31
- edge_inputs: bfloat16 [294912, 1536], P(('rep', 'sp')), may hold values from -24 to 24
- cotangent: bfloat16 [294912, 512], P(('rep', 'sp')), may hold values from -0.15625 to 0.15625
Outputs:
- hidden: bfloat16 [192, 32, 100, 128], P('rep', 'sp')
- weight_grad: float32 [1536, 512], P(('rep', 'sp'))
Inputs may be any that keep to these rules, and one draw needn't show every extreme that they name: `send_count`: every count is at most 8, and some pair of shards has exactly 8 in every draw.
All inputs are finite; a program needn't handle non-finite values.
Results may differ from a plain program's by a relative error of at most 0.001.
Values may be sent and summed in bfloat16 or wider, within the bound.
A program may use at most 32 MiB of HBM per device.

v0:
```python
import jax
import jax.numpy as jnp
from jax import lax
from jax.sharding import Mesh
from jax.sharding import PartitionSpec as P

SP = ("sp_0", "sp_1")
REP_SP = ("rep_0", "rep_1", "rep_2", "sp_0", "sp_1")
REP = ("rep_0", "rep_1", "rep_2")


def split_up(value, dim, length):
    lengths = value.shape
    tiles = value.reshape(*lengths[:dim], length, lengths[dim] // length, *lengths[dim + 1 :])
    return jnp.moveaxis(tiles, dim, 0)


def edges_of(length, count):
    lap = length // count
    if lap >= 8:
        lap -= lap % 8
    return [lap * k for k in range(1, count)]


def reduced_to_own(tiles, axes, turns):
    inside = tiles.shape[1:]
    tiles = tiles.reshape(*(lax.axis_size(a) for a in axes), *inside)
    tiles = jnp.moveaxis(tiles, turns, range(len(axes))).reshape(-1, *inside)
    for k in turns:
        tiles = lax.psum_scatter(tiles, axes[k], scatter_dimension=0, tiled=True)
    return tiles[0]


def spread_scatter(value, axes, dim):
    tiles = split_up(value, dim, lax.axis_size(axes))
    cut = max(range(1, max(2, tiles.ndim - 1)), key=lambda d: tiles.shape[d])
    count, outs = (len(axes), [])
    for leading, slab in enumerate(jnp.split(tiles, edges_of(tiles.shape[cut], count), axis=cut)):
        if slab.size:
            turns = [(leading + k) % count for k in range(count)]
            outs.append(reduced_to_own(slab, axes, turns))
    return jnp.concatenate(outs, axis=cut - 1)


def body(field, send_blocks, send_count, regrid_weights, tile_slot, edge_inputs, cotangent):
    sample = field[0]
    own_lists = send_blocks[0]
    shards = own_lists.shape[0]
    slots_each = own_lists.shape[1]
    channels = sample.shape[1]
    cells = sample.shape[2]
    alive = jnp.arange(slots_each, dtype=jnp.int32)[None, :] < send_count[0][:, None]
    outgoing = jnp.where(alive[:, :, None, None], sample[own_lists], jnp.zeros((), jnp.bfloat16))
    incoming = lax.all_to_all(outgoing, SP, split_axis=0, concat_axis=0, tiled=True)
    block_pool = incoming.reshape(shards * slots_each, channels, cells)
    reads = tile_slot.shape[1]
    selector = (
        tile_slot.reshape(-1)[:, None] == jnp.arange(shards * slots_each, dtype=jnp.int32)[None, :]
    ).astype(jnp.bfloat16)
    flat_pool = block_pool.reshape(shards * slots_each, channels * cells)
    picked = jnp.dot(selector, flat_pool, preferred_element_type=jnp.float32).astype(jnp.bfloat16)
    picked = picked.reshape(tile_slot.shape[0], reads, channels, cells)
    hidden = jnp.einsum(
        "tbcx,tbxn->tcn", picked, regrid_weights, preferred_element_type=jnp.float32
    )
    hidden = hidden.astype(jnp.bfloat16)[None]
    weight_grad = spread_scatter(
        lax.dot_general(
            edge_inputs, cotangent, (((0,), (0,)), ((), ())), preferred_element_type=jnp.float32
        ),
        REP_SP,
        0,
    )
    return (hidden, weight_grad)


def solution(mesh):
    split = Mesh(mesh.devices.reshape(8, 4, 6, 2, 2), ("rep_0", "rep_1", "rep_2", "sp_0", "sp_1"))
    return jax.shard_map(
        body,
        mesh=split,
        in_specs=(
            P(REP, SP, None, None),
            P(SP, None, None),
            P(SP, None),
            P(SP, None, None, None),
            P(SP, None),
            P(REP_SP, None),
            P(REP_SP, None),
        ),
        out_specs=(P(REP, SP, None, None), P(REP_SP, None)),
        check_vma=False,
    )
```

profile of v0, /device:TPU:8, one launch (start us, length us, event | category | flops | bytes accessed | tf_op | source)
XLA Modules:
  0.0 282.2 jit_solution(6613692708527782639)
XLA Ops:
  7.2 0.0 all-reduce.9.cloned.1.call-start
  7.2 4.2 %fusion.14 = f32[1536,512]{1,0:T(8,128)} fusion(bf16[384,1536]{1,0:T(8,128)(2,1)} %param.12, bf16[384,512]{1,0:T(8,128)(2,1)} %param.13), kind=kOutput, calls=%fused_computation.21 | convolution fusion | flops 603979776 | bytes 4718592 | tf_op jit(solution)/shard_map/dot_general | solution.py:68
  11.4 5.2 %reshape_reshape.7 = f32[8,4,6,2,2,2,512]{6,5,4,3,2,1,0:T(2,128)} reshape(f32[1536,512]{1,0:T(8,128)} %fusion.14) | data formatting | bytes 6291456 | tf_op jit(solution)/shard_map/reshape;reshape | solution.py:27
  16.6 5.5 %copy.20 = f32[2,8,4,6,2,2,512]{6,5,4,3,2,1,0:T(2,128)} copy(f32[2,8,4,6,2,2,512]{6,5,0,4,3,2,1:T(2,128)} %bitcast.36) | data formatting | bytes 6291456 | tf_op jit(solution)/shard_map/transpose | solution.py:28
  22.1 0.0 all-reduce.9.cloned.1.call-update
  22.1 1.5 copy.33
  23.6 0.1 reshape.67
  23.7 1.6 gather_fusion
  25.3 0.1 iota_compare_fusion.2
  25.4 2.2 copy_select_fusion
  27.6 14.5 %all-to-all-start = ((bf16[4,8,100,128]{3,1,2,0:T(8,128)(2,1)}), bf16[4,8,100,128]{3,1,2,0:T(8,128)(2,1)S(1)}, u32[]{:S(2)}, u32[]{:S(2)}) async-start(bf16[4,8,100,128]{3,1,2,0:T(8,128)(2,1)} %copy_select_fusion), calls=%async_computation | async-start | bytes 1638400 | tf_op jit(solution)/shard_map/all_to_all | solution.py:54
  42.1 1.3 dynamic-slice
  44.0 30.2 %all-reduce.9.cloned.1.call-done = f32[768,2,512]{2,1,0:T(2,128)} async-done(((f32[768,2,512]{2,1,0:T(2,128)}), f32[768,2,512]{2,1,0:T(2,128)}) %all-reduce.9.cloned.1.call-update) | async-done | bytes 3145744
  74.2 3.1 %constant_dynamic-slice_fusion.3 = f32[384,2,512]{2,1,0:T(2,128)} fusion(f32[768,2,512]{2,1,0:T(2,128)} %all-reduce.9.cloned.1.call-done, u32[]{:T(128)S(6)} %multiply.1), kind=kLoop, calls=%fused_computation.20 | loop fusion | bytes 3145732
  77.3 0.0 all-reduce.11.cloned.1.call-update
  77.3 0.0 all-reduce.13.cloned.1.call-start
  77.3 1.3 dynamic-slice.2
  78.6 1.3 dynamic-slice.4
  79.9 1.3 dynamic-slice.6
  81.1 1.3 dynamic-slice.8
  82.4 0.1 eq.15
  84.4 1.8 fusion.2
  86.2 81.5 %all-reduce.11.cloned.1.call-done = f32[384,2,512]{2,1,0:T(2,128)} async-done(((f32[384,2,512]{2,1,0:T(2,128)}), f32[384,2,512]{2,1,0:T(2,128)}) %all-reduce.11.cloned.1.call-update) | async-done | bytes 1572880
  167.7 1.6 constant_dynamic-slice_fusion.2
  169.3 0.0 all-reduce.13.cloned.1.call-update
  169.4 2.0 fusion.9
  171.4 0.7 copy.21
  172.1 55.8 %all-reduce.13.cloned.1.call-done = f32[48,2,512]{2,1,0:T(2,128)} async-done(((f32[48,2,512]{2,1,0:T(2,128)}), f32[48,2,512]{2,1,0:T(2,128)}) %all-reduce.13.cloned.1.call-update) | async-done | bytes 196624
  228.0 0.8 constant_dynamic-slice_fusion.1
  228.8 34.3 %all-reduce.3 = f32[12,2,512]{2,1,0:T(2,128)S(1)} all-reduce(f32[12,2,512]{2,1,0:T(2,128)S(1)} %constant_dynamic-slice_fusion.1), channel_id=5, replica_groups=mesh['rep_0'=8,'rep_1'=4,'rep_2'=6,'sp_0'=2,'sp_1'=2] {'rep_2'}, use_global_device_ids=true, to_apply=%region_3.4.clone | all-reduce | flops 12288 | bytes 98304
  263.1 11.3 %all-reduce.4 = f32[2,2,512]{2,1,0:T(2,128)S(1)} all-reduce(f32[2,2,512]{2,1,0:T(2,128)S(1)} %constant_dynamic-slice_fusion), channel_id=6, replica_groups=mesh['rep_0'=8,'rep_1'=4,'rep_2'=6,'sp_0'=2,'sp_1'=2] {'sp_0'}, use_global_device_ids=true, to_apply=%region_4.5.clone | all-reduce | flops 2048 | bytes 16384
  274.4 1.2 dynamic-slice_bitcast_fusion
  (13 shorter events, 0.1 us)
Async XLA Ops:
  7.2 162.2 %copy-start = (bf16[8,8,128,128]{3,2,1,0:T(8,128)(2,1)S(1)}, bf16[8,8,128,128]{3,2,1,0:T(8,128)(2,1)}, u32[]{:S(2)}) copy-start(bf16[8,8,128,128]{3,2,1,0:T(8,128)(2,1)} %param.10) | copy-start | bytes 6291460
  7.2 67.0 %all-reduce.9.cloned.1.call-start = ((), (), s32[]{:S(2)}) async-start(), calls=%async_computation.1 | async-start | bytes 6291456
  22.1 1.5 copy-start.2
  22.1 3.2 %copy-start.3 = (s32[1,4]{1,0:T(1,128)S(1)}, s32[1,4]{1,0:T(1,128)}, u32[]{:S(2)}) copy-start(s32[1,4]{1,0:T(1,128)} %param.9) | copy-start | bytes 52
  27.6 56.8 %all-to-all-start = ((bf16[4,8,100,128]{3,1,2,0:T(8,128)(2,1)}), bf16[4,8,100,128]{3,1,2,0:T(8,128)(2,1)S(1)}, u32[]{:S(2)}, u32[]{:S(2)}) async-start(bf16[4,8,100,128]{3,1,2,0:T(8,128)(2,1)} %copy_select_fusion), calls=%async_computation | async-start | bytes 1638400 | tf_op jit(solution)/shard_map/all_to_all | solution.py:54
  42.1 125.7 %all-reduce.11.cloned.1.call-start = ((), (), s32[]{:S(2)}) async-start(), calls=%async_computation.2 | async-start | bytes 3145728
  44.0 38.4 %copy-start.1 = (s32[8,8]{1,0:T(8,128)S(1)}, s32[8,8]{1,0:T(8,128)}, u32[]{:S(2)}) copy-start(s32[8,8]{1,0:T(8,128)} %param.11) | copy-start | bytes 772
  77.3 150.7 %all-reduce.13.cloned.1.call-start = ((), (), s32[]{:S(2)}) async-start(), calls=%async_computation.3 | async-start | bytes 393216
Sparse Core Ops, SparseCore 0:
  22.3 51.8 all-reduce.8
  77.4 90.2 all-reduce.10
  170.0 57.8 all-reduce.12
where the time goes:
time: 283 us; the launch traced here: 282 us
  waiting for transfers between devices  168 us (59%)
  blocking collectives  45.7 us (16%)
  local copies, waits for them, and re-layouts  27.7 us (10%)
  between operations  16.3 us (6%)
  starting transfers between devices  14.6 us (5%)
  matrix products  8.06 us (3%)
    unnamed x6, waiting for transfers between devices  168 us
    unnamed x2, blocking collectives  45.7 us
    all_to_all x1, starting transfers between devices, body(): lax.all_to_all(outgoing, SP, split_axis=0, concat_axis=0, tiled=True)  14.5 us
    unnamed x19, local copies, waits for them, and re-layouts  14.1 us
  transfers between devices with their start and end apart: 4, of which 3 were waited for; matrix products, arithmetic and copies ran while one was open for 7% of the time, Pallas kernels for 0%

commit v1 on v0

v1 whole, which is shorter than its diff:
```python
import jax
import jax.numpy as jnp
from jax import lax
from jax.experimental import pallas as pl
from jax.experimental.pallas import tpu as pltpu
from jax.sharding import Mesh
from jax.sharding import PartitionSpec as P

AXES = ("y", "x", "zl", "zh", "c")
NY, NX, NZL, NZH, NC = 8, 4, 6, 2, 2
NZ = NZL * NZH
ROWS = 48
XROWS = 40
MESH = pl.DeviceIdType.MESH


def kernel(
    blocks_ref, count_ref, slot_ref, field_hbm, weights_hbm, edges_hbm, cot_hbm,
    hidden_ref, grad_ref,
    field, weights, edges, cot, outgoing, pool,
    part, given, chip, from_x, sum_x, from_y, last_y, sum_y, last_x, total, to_z, from_z,
    in_sem, a_send, a_recv, d_send, d_recv, x_send, x_recv, y_send, y_recv,
    u_send, u_recv, v_send, v_recv, z_send, z_recv,
):
    y, x = lax.axis_index("y"), lax.axis_index("x")
    zl, zh, c = lax.axis_index("zl"), lax.axis_index("zh"), lax.axis_index("c")
    z = zh * NZL + zl
    own = zh * NC + c
    half = cot.shape[1] // 2

    def at(dy=0, dx=0, dz=0, dc=0):
        other = lax.rem(z + dz, NZ)
        return (
            lax.rem(y + dy, NY), lax.rem(x + dx, NX),
            lax.rem(other, NZL), lax.div(other, NZL), lax.rem(c + dc, NC),
        )

    loads = [
        pltpu.make_async_copy(field_hbm.at[0], field, in_sem.at[0]),
        pltpu.make_async_copy(edges_hbm, edges, in_sem.at[1]),
        pltpu.make_async_copy(cot_hbm, cot, in_sem.at[2]),
        pltpu.make_async_copy(weights_hbm, weights, in_sem.at[3]),
    ]
    for load in loads:
        load.start()

    barrier = pltpu.get_barrier_semaphore()

    def greet(**offset):
        pl.semaphore_signal(barrier, inc=1, device_id=at(**offset), device_id_type=MESH)

    def greet_z(k, carry):
        greet(dz=k)
        greet(dz=k, dc=1)
        return carry

    def greet_y(k, carry):
        greet(dy=k)
        return carry

    lax.fori_loop(1, NZ, greet_z, 0)
    lax.fori_loop(1, NY, greet_y, 0)
    for k in range(1, NX):
        greet(dx=k)
    greet(dc=1)

    loads[0].wait()

    def picked(shard, j):
        block = field[blocks_ref[0, shard, j]]
        return jnp.where(j < count_ref[0, shard], block, jnp.zeros_like(block))

    shard_of = [lax.rem(zh + k // 2, NZH) * NC + lax.rem(c + k % 2, NC) for k in range(4)]

    def gather(j, carry):
        for k in (2, 3, 1):
            outgoing[k - 1, j] = picked(shard_of[k], j)
        pool[own * 8 + j] = picked(own, j)
        return carry

    lax.fori_loop(0, 8, gather, 0)

    loads[1].wait()
    loads[2].wait()
    for k in range(4):
        piece = lax.dot_general(
            edges[:, k * 384 : (k + 1) * 384], cot[...], (((0,), (0,)), ((), ())),
            preferred_element_type=jnp.float32,
        )
        for h in range(2):
            part[h, 2 * k : 2 * k + 2] = piece[:, h * half : (h + 1) * half].reshape(2, NX, ROWS, half)

    pl.semaphore_wait(barrier, 2 * (NZ - 1) + (NY - 1) + (NX - 1) + 1)

    def block_copy(k):
        return pltpu.make_async_remote_copy(
            src_ref=outgoing.at[k - 1], dst_ref=pool.at[pl.ds(own * 8, 8)],
            send_sem=a_send.at[k - 1], recv_sem=a_recv.at[k - 1],
            device_id=at(dz=NZL * (k // 2), dc=k % 2), device_id_type=MESH,
        )

    for k in (2, 3, 1):
        block_copy(k).start()

    def away(k):
        return 4 + lax.div(k, 2) * (1 - 2 * lax.rem(k, 2)) - lax.rem(k, 2)

    def core_copy(dy):
        return pltpu.make_async_remote_copy(
            src_ref=part.at[1 - c, lax.rem(y + dy, NY)], dst_ref=given.at[dy],
            send_sem=d_send.at[dy], recv_sem=d_recv.at[dy], device_id=at(dc=1), device_id_type=MESH,
        )

    def x_copy(dx, dy):
        return pltpu.make_async_remote_copy(
            src_ref=chip.at[dy, lax.rem(x + dx, NX), pl.ds(0, XROWS)], dst_ref=from_x.at[dx - 1, dy],
            send_sem=x_send.at[dx - 1, dy], recv_sem=x_recv.at[dx - 1, dy],
            device_id=at(dx=dx), device_id_type=MESH,
        )

    def y_copy(dy):
        return pltpu.make_async_remote_copy(
            src_ref=sum_x.at[dy], dst_ref=from_y.at[dy], send_sem=y_send.at[dy], recv_sem=y_recv.at[dy],
            device_id=at(dy=dy), device_id_type=MESH,
        )

    def u_copy(dy):
        return pltpu.make_async_remote_copy(
            src_ref=chip.at[dy, :, pl.ds(XROWS, ROWS - XROWS)], dst_ref=last_y.at[dy],
            send_sem=u_send.at[dy], recv_sem=u_recv.at[dy], device_id=at(dy=dy), device_id_type=MESH,
        )

    def v_copy(dx):
        return pltpu.make_async_remote_copy(
            src_ref=sum_y.at[lax.rem(x + dx, NX)], dst_ref=last_x.at[dx - 1],
            send_sem=v_send.at[dx - 1], recv_sem=v_recv.at[dx - 1], device_id=at(dx=dx), device_id_type=MESH,
        )

    def start_core(k, carry):
        core_copy(away(k)).start()
        return carry

    lax.fori_loop(0, NY, start_core, 0)

    def send_x(k):
        dy = away(k)
        for dx in (2, 1, 3):
            x_copy(dx, dy).start()

        @pl.when(dy > 0)
        def _():
            u_copy(dy).start()

    def over_cores(k, carry):
        dy = away(k)
        core_copy(dy).wait_recv()
        chip[dy] = part[c, lax.rem(y + dy, NY)] + given[dy]

        @pl.when(k > 0)
        def _():
            send_x(k - 1)

        return carry

    lax.fori_loop(0, NY, over_cores, 0)
    send_x(NY - 1)

    def send_y(k):
        dy = away(k)

        @pl.when(dy > 0)
        def _():
            y_copy(dy).start()

    def over_x(k, carry):
        dy = away(k)
        for dx in (1, 3, 2):
            x_copy(dx, dy).wait_recv()
        sum_x[dy] = chip[dy, x, :XROWS] + from_x[0, dy] + from_x[1, dy] + from_x[2, dy]

        @pl.when(k > 0)
        def _():
            send_y(k - 1)

        return carry

    lax.fori_loop(0, NY, over_x, 0)

    rest = chip[0, :, XROWS:]
    for dy in range(1, NY):
        u_copy(dy).wait_recv()
        rest = rest + last_y[dy]
    sum_y[...] = rest

    result = sum_x[0]
    for dy in range(1, NY):
        y_copy(dy).wait_recv()
        result = result + from_y[dy]
    total[:XROWS] = result
    for dx in (2, 1, 3):
        v_copy(dx).start()
    rest = sum_y[x]
    for dx in (1, 3, 2):
        v_copy(dx).wait_recv()
        rest = rest + last_x[dx - 1]
    total[XROWS:] = rest

    for low in range(NZL):
        tile = total[low * 8 : low * 8 + 8]
        for high in range(NZH):
            for core in range(NC):
                row = high * 4 + core * 2
                to_z[high * NZL + low, core] = tile[row : row + 2]

    def z_copy(dz, dc):
        core = lax.rem(c + dc, NC)
        return pltpu.make_async_remote_copy(
            src_ref=to_z.at[lax.rem(z + dz, NZ), core], dst_ref=from_z.at[dz, c],
            send_sem=z_send.at[dz, dc], recv_sem=z_recv.at[dz, dc],
            device_id=at(dz=dz, dc=dc), device_id_type=MESH,
        )

    from_z[0, c] = to_z[z, c]

    def start_z(k, carry):
        z_copy(k, 0).start()
        z_copy(k, 1).start()
        return carry

    lax.fori_loop(1, NZ, start_z, 0)
    z_copy(0, 1).start()

    loads[3].wait()
    for k in (1, 2, 3):
        block_copy(k).wait_recv()

    def tile_of(t, carry):
        left = jnp.concatenate([pool[slot_ref[t, b]] for b in range(8)], axis=1)
        right = weights[t].reshape(-1, weights.shape[-1])
        hidden_ref[0, t] = jnp.dot(left, right, preferred_element_type=jnp.float32).astype(jnp.bfloat16)
        return carry

    lax.fori_loop(0, 8, tile_of, 0)

    def wait_z(dz, dc):
        pltpu.make_async_remote_copy(
            src_ref=to_z.at[0, 0], dst_ref=from_z.at[dz, lax.rem(c + dc, NC)],
            send_sem=z_send.at[dz, dc], recv_sem=z_recv.at[dz, dc],
            device_id=at(dz=dz, dc=dc), device_id_type=MESH,
        ).wait_recv()

    def end_z(k, carry):
        wait_z(k, 0)
        wait_z(k, 1)
        return carry

    lax.fori_loop(1, NZ, end_z, 0)
    wait_z(0, 1)
    for core in range(NC):
        value = from_z[0, core]
        for dz in range(1, NZ):
            value = value + from_z[dz, core]
        grad_ref[:, core * half : (core + 1) * half] = value

    for k in (1, 2, 3):
        block_copy(k).wait_send()

    def drain_y(dy, carry):
        core_copy(dy).wait_send()
        for dx in (1, 2, 3):
            x_copy(dx, dy).wait_send()

        @pl.when(dy > 0)
        def _():
            y_copy(dy).wait_send()
            u_copy(dy).wait_send()

        return carry

    lax.fori_loop(0, NY, drain_y, 0)
    for dx in (1, 2, 3):
        v_copy(dx).wait_send()

    def drain_z(k, carry):
        z_copy(k, 0).wait_send()
        z_copy(k, 1).wait_send()
        return carry

    lax.fori_loop(1, NZ, drain_z, 0)
    z_copy(0, 1).wait_send()


def body(field, send_blocks, send_count, regrid_weights, tile_slot, edge_inputs, cotangent):
    tiles, reads, cells, nodes = regrid_weights.shape
    channels = field.shape[2]
    half = cotangent.shape[1] // 2
    f32, bf16 = jnp.float32, jnp.bfloat16
    dma = pltpu.SemaphoreType.DMA
    smem = pl.BlockSpec(memory_space=pltpu.SMEM)
    vmem = pl.BlockSpec(memory_space=pltpu.VMEM)
    hbm = pl.BlockSpec(memory_space=pl.ANY)
    return pl.pallas_call(
        kernel,
        name="regrid",
        out_shape=(
            jax.ShapeDtypeStruct((1, tiles, channels, nodes), bf16),
            jax.ShapeDtypeStruct((2, 2 * half), f32),
        ),
        in_specs=[smem, smem, smem, hbm, hbm, hbm, hbm],
        out_specs=(vmem, vmem),
        scratch_shapes=[
            pltpu.VMEM(field.shape[1:], bf16),
            pltpu.VMEM(regrid_weights.shape, bf16),
            pltpu.VMEM(edge_inputs.shape, bf16),
            pltpu.VMEM(cotangent.shape, bf16),
            pltpu.VMEM((3, 8, channels, cells), bf16),
            pltpu.VMEM((32, channels, cells), bf16),
            pltpu.VMEM((2, NY, NX, ROWS, half), f32),
            pltpu.VMEM((NY, NX, ROWS, half), f32),
            pltpu.VMEM((NY, NX, ROWS, half), f32),
            pltpu.VMEM((NX - 1, NY, XROWS, half), f32),
            pltpu.VMEM((NY, XROWS, half), f32),
            pltpu.VMEM((NY, XROWS, half), f32),
            pltpu.VMEM((NY, NX, ROWS - XROWS, half), f32),
            pltpu.VMEM((NX, ROWS - XROWS, half), f32),
            pltpu.VMEM((NX - 1, ROWS - XROWS, half), f32),
            pltpu.VMEM((ROWS, half), f32),
            pltpu.VMEM((NZ, NC, 2, half), f32),
            pltpu.VMEM((NZ, NC, 2, half), f32),
            dma((4,)),
            dma((3,)), dma((3,)),
            dma((NY,)), dma((NY,)),
            dma((NX - 1, NY)), dma((NX - 1, NY)),
            dma((NY,)), dma((NY,)),
            dma((NY,)), dma((NY,)),
            dma((NX - 1,)), dma((NX - 1,)),
            dma((NZ, NC)), dma((NZ, NC)),
        ],
        compiler_params=pltpu.CompilerParams(
            collective_id=0, has_side_effects=True, vmem_limit_bytes=56 * 2**20
        ),
    )(send_blocks, send_count, tile_slot, field, regrid_weights, edge_inputs, cotangent)


def solution(mesh):
    split = Mesh(mesh.devices.reshape(NY, NX, NZL, NZH, NC), AXES)
    rep, sp = AXES[:3], AXES[3:]
    return jax.shard_map(
        body,
        mesh=split,
        in_specs=(
            P(rep, sp, None, None),
            P(sp, None, None),
            P(sp, None),
            P(sp, None, None, None),
            P(sp, None),
            P(AXES, None),
            P(AXES, None),
        ),
        out_specs=(P(rep, sp, None, None), P(AXES, None)),
        check_vma=False,
    )
```

time: 283 us -> 61.6 us (0.22)
  the two profiles are of different devices: /device:TPU:8 before, /device:TPU:1 now
where the time goes in v1:
time: 61.6 us; the launch traced here: 61.3 us
  Pallas kernels  55.4 us (90%)
  local copies, waits for them, and re-layouts  5.28 us (9%)
  between operations  0.64 us (1%)
    pallas_call x1, Pallas kernels, body(): pl.pallas_call(kernel, name='regrid', out_shape=(jax.ShapeDtypeStruct((1,...  55.4 us
    unnamed x2, local copies, waits for them, and re-layouts  3.63 us
    pallas_call x1, local copies, waits for them, and re-layouts, body(): pl.pallas_call(kernel, name='regrid', out_shape=(jax.ShapeDtypeStruct((1,...  1.64 us

profile of v1, /device:TPU:1, one launch (start us, length us, event | category | flops | bytes accessed | tf_op | source)
XLA Modules:
  0.0 61.3 jit_solution(15590792881352695624)
XLA Ops:
  0.6 2.4 %copy.9.field_hbm = bf16[1,32,100,128]{3,2,1,0:T(8,128)(2,1)} copy(bf16[1,32,100,128]{3,1,2,0:T(8,128)(2,1)} %param.7) | data formatting | bytes 1638400 | tf_op args[0]
  3.0 55.4 %regrid.1 = (bf16[1,8,100,128]{3,2,1,0:T(8,128)(2,1)}, f32[2,512]{1,0:T(2,128)}) custom-call(s32[1,4,8]{2,1,0:T(4,128)} %blocks_ref.1, s32[1,4]{1,0:T(1,128)} %count_ref.1, s32[8,8]{1,0:T(8,128)} %slot_ref.1, bf16[1,32,100,128]{3,2,1,0:T(8,128)(2,1)} %copy.9.field_hbm, bf16[8,8,128,128]{3,2,1,0:T(8,128)(2,1)} %weights_hbm.1, bf16[384,1536]{1,0:T(8,128)(2,1)} %edges_hbm.1, ...), custom_call_target="tpu_custom_call" | custom-call | tf_op jit(solution)/shard_map/regrid/pallas_call | solution.py:302
  58.4 1.6 %copy.10 = bf16[1,8,100,128]{3,1,2,0:T(8,128)(2,1)} copy(bf16[1,8,100,128]{3,2,1,0:T(8,128)(2,1)} %get-tuple-element.2) | data formatting | bytes 409600 | tf_op jit(solution)/shard_map/regrid/pallas_call | solution.py:302
  60.1 1.3 %copy.12 = f32[2,512]{1,0:T(2,128)} copy(f32[2,512]{1,0:T(2,128)} %get-tuple-element.7) | data formatting | bytes 8192

commit v2 on v1

v2 whole, which is shorter than its diff:
```python
import jax
import jax.numpy as jnp
from jax import lax
from jax.experimental import pallas as pl
from jax.experimental.pallas import tpu as pltpu
from jax.sharding import Mesh
from jax.sharding import PartitionSpec as P

AXES = ("y", "x", "zl", "zh", "c")
NY, NX, NZL, NZH, NC = 8, 4, 6, 2, 2
NZ = NZL * NZH
LANES = 128
ROWS = 96
FIRST = 80
MAIN = 96
PITCH = 40
XROWS = 72
MESH = pl.DeviceIdType.MESH


def kernel(
    blocks_hbm, count_hbm, slot_hbm, field_hbm, weights_hbm, edges_hbm, cot_hbm,
    hidden_ref, grad_ref,
    blocks_ref, count_ref, slot_ref, field, wide, weights, edges, cot,
    out_a, out_b, out_tail, pool_a, pool_b, pool_tail, tails, nodes,
    part, given, chip, from_x, sum_x, from_y, last_y, sum_y, last_x, total, to_z, from_z,
    in_sem, a_send, a_recv, d_send, d_recv, x_send, x_recv, y_send, y_recv,
    u_send, u_recv, v_send, v_recv, z_send, z_recv,
):
    y, x = lax.axis_index("y"), lax.axis_index("x")
    zl, zh, c = lax.axis_index("zl"), lax.axis_index("zh"), lax.axis_index("c")
    z = zh * NZL + zl
    own = zh * NC + c
    half = cot.shape[1] // 2

    def at(dy=0, dx=0, dz=0, dc=0):
        other = lax.rem(z + dz, NZ)
        return (
            lax.rem(y + dy, NY), lax.rem(x + dx, NX),
            lax.rem(other, NZL), lax.div(other, NZL), lax.rem(c + dc, NC),
        )

    loads = [
        pltpu.make_async_copy(source, goal, in_sem.at[k])
        for k, (source, goal) in enumerate(
            (
                (field_hbm, field), (edges_hbm, edges), (cot_hbm, cot), (weights_hbm, weights),
                (blocks_hbm, blocks_ref), (count_hbm, count_ref), (slot_hbm, slot_ref),
            )
        )
    ]

    barrier = pltpu.get_barrier_semaphore()

    def greet(**offset):
        pl.semaphore_signal(barrier, inc=1, device_id=at(**offset), device_id_type=MESH)

    for k in (6, 5, 7, 4, 8, 3, 9, 2, 10, 1, 11):
        greet(dz=k)
        greet(dz=k, dc=1)
        if k == 6:
            for load in loads:
                load.start()
    for k in (4, 3, 5, 2, 6, 1, 7):
        greet(dy=k)
    for k in (2, 1, 3):
        greet(dx=k)
    greet(dc=1)

    for k in (0, 4, 5):
        loads[k].wait()

    def widen(k, carry):
        for i in range(10):
            row = k * 10 + i
            wide[pl.ds(pl.multiple_of(row * PITCH, 8), 32)] = field[pl.ds(pl.multiple_of(row * 32, 32), 32)].astype(
                jnp.float32
            )
        return carry

    lax.fori_loop(0, 10, widen, 0)

    def gather(i, carry):
        k = lax.rem(i + 2, 4)
        shard = lax.rem(zh + lax.div(k, 2), NZH) * NC + lax.rem(c + lax.rem(k, 2), NC)
        last = []
        for j in range(8):
            start = blocks_ref[0, shard, j]
            alive = j < count_ref[0, shard]
            main = wide[pl.ds(start, MAIN, stride=PITCH)]
            main = jnp.where(alive, main, jnp.zeros_like(main)).astype(jnp.bfloat16)
            out_a[k, j] = main[:FIRST]
            out_b[k, j] = main[FIRST:]
            tail = wide[pl.ds(start + MAIN * PITCH, 4, stride=PITCH)]
            last.append(jnp.where(alive, tail, jnp.zeros_like(tail)))
        out_tail[k] = jnp.concatenate(last, axis=0).astype(jnp.bfloat16)
        return carry

    lax.fori_loop(0, 4, gather, 0)
    pool_a[pl.ds(own * 8, 8)] = out_a[0]
    pool_b[pl.ds(own * 8, 8)] = out_b[0]
    pool_tail[own] = out_tail[0]

    loads[1].wait()
    loads[2].wait()
    for k in range(4):
        piece = lax.dot_general(
            edges[:, k * 384 : (k + 1) * 384], cot[...], (((0,), (0,)), ((), ())),
            preferred_element_type=jnp.float32,
        )
        for h in range(2):
            for g in range(2):
                column = h * half + g * LANES
                part[h, 2 * k : 2 * k + 2, :, g * 48 : g * 48 + 48] = piece[:, column : column + LANES].reshape(
                    2, NX, 48, LANES
                )

    pl.semaphore_wait(barrier, 2 * (NZ - 1) + (NY - 1) + (NX - 1) + 1)

    def remote(source, goal, send, recv, **offset):
        return pltpu.make_async_remote_copy(
            src_ref=source, dst_ref=goal, send_sem=send, recv_sem=recv,
            device_id=at(**offset), device_id_type=MESH,
        )

    def block_copy(k, kind):
        source, goal = (
            (out_a.at[k], pool_a.at[pl.ds(own * 8, 8)]),
            (out_tail.at[k], pool_tail.at[own]),
            (out_b.at[k], pool_b.at[pl.ds(own * 8, 8)]),
        )[kind]
        return remote(source, goal, a_send.at[kind], a_recv.at[kind], dz=NZL * (k // 2), dc=k % 2)

    def all_blocks(kind):
        whole = (pool_a.at[pl.ds(0, 24)], pool_tail.at[pl.ds(0, 3)], pool_b.at[pl.ds(0, 24)])[kind]
        return remote(whole, whole, a_send.at[kind], a_recv.at[kind], dc=1)

    for k in (2, 3):
        for kind in (0, 1):
            block_copy(k, kind).start()
    for kind in range(3):
        block_copy(1, kind).start()

    def away(k):
        return 4 + lax.div(k, 2) * (1 - 2 * lax.rem(k, 2)) - lax.rem(k, 2)

    def core_copy(dy):
        return remote(
            part.at[1 - c, lax.rem(y + dy, NY)], given.at[dy], d_send.at[0], d_recv.at[dy], dc=1
        )

    def x_copy(dx, dy):
        return remote(
            chip.at[dy, lax.rem(x + dx, NX), pl.ds(0, XROWS)], from_x.at[dy, dx - 1],
            x_send.at[0], x_recv.at[dy], dx=dx,
        )

    def y_copy(dy):
        return remote(sum_x.at[dy], from_y.at[dy], y_send.at[0], y_recv.at[0], dy=dy)

    def u_copy(dy):
        return remote(
            chip.at[dy, :, pl.ds(XROWS, ROWS - XROWS)], last_y.at[dy], u_send.at[0], u_recv.at[0], dy=dy
        )

    def v_copy(dx):
        return remote(sum_y.at[lax.rem(x + dx, NX)], last_x.at[dx - 1], v_send.at[0], v_recv.at[0], dx=dx)

    def all_of(whole, send, recv):
        return remote(whole, whole, send, recv, dc=1)

    all_x = all_of(from_x, x_send.at[0], x_recv.at[0])
    all_y = all_of(from_y.at[pl.ds(1, NY - 1)], y_send.at[0], y_recv.at[0])
    all_u = all_of(last_y.at[pl.ds(1, NY - 1)], u_send.at[0], u_recv.at[0])
    all_v = all_of(last_x, v_send.at[0], v_recv.at[0])

    def start_core(k, carry):
        core_copy(away(k)).start()
        return carry

    lax.fori_loop(0, NY, start_core, 0)

    def send_x(k):
        dy = away(k)
        for dx in (2, 1, 3):
            x_copy(dx, dy).start()

        @pl.when(dy > 0)
        def _():
            u_copy(dy).start()

    def over_cores(k, carry):
        dy = away(k)
        core_copy(dy).wait_recv()
        chip[dy] = part[c, lax.rem(y + dy, NY)] + given[dy]

        @pl.when(k > 0)
        def _():
            send_x(k - 1)

        return carry

    lax.fori_loop(0, NY, over_cores, 0)
    send_x(NY - 1)

    def send_y(k):
        dy = away(k)

        @pl.when(dy > 0)
        def _():
            y_copy(dy).start()

    def over_x(k, carry):
        dy = away(k)
        all_of(from_x.at[dy], x_send.at[0], x_recv.at[dy]).wait_recv()
        sum_x[dy] = chip[dy, x, :XROWS] + from_x[dy, 0] + from_x[dy, 1] + from_x[dy, 2]

        @pl.when(k > 0)
        def _():
            send_y(k - 1)

        return carry

    lax.fori_loop(0, NY, over_x, 0)

    rest = chip[0, :, XROWS:]
    all_u.wait_recv()
    for dy in range(1, NY):
        rest = rest + last_y[dy]
    sum_y[...] = rest

    result = sum_x[0]
    for dx in (2, 1, 3):
        v_copy(dx).start()
    all_y.wait_recv()
    for dy in range(1, NY):
        result = result + from_y[dy]
    total[:XROWS] = result
    rest = sum_y[x]
    all_v.wait_recv()
    for dx in range(1, NX):
        rest = rest + last_x[dx - 1]
    total[XROWS:] = rest

    for low in range(NZL):
        for group in range(2):
            tile = total[group * 48 + low * 8 : group * 48 + low * 8 + 8]
            for high in range(NZH):
                for core in range(NC):
                    row = high * 4 + core * 2
                    to_z[(high * NZL + low) * NC + core, :, group * LANES : (group + 1) * LANES] = tile[row : row + 2]

    def z_copy(dz, dc):
        return remote(
            to_z.at[lax.rem(z + dz, NZ) * NC + lax.rem(c + dc, NC)], from_z.at[dz * NC + c],
            z_send.at[0], z_recv.at[0], dz=dz, dc=dc,
        )

    all_z = all_of(from_z.at[pl.ds(0, NZ * NC - 1)], z_send.at[0], z_recv.at[0])
    from_z[c] = to_z[z * NC + c]

    def start_z(k, carry):
        z_copy(k, 0).start()
        z_copy(k, 1).start()
        return carry

    lax.fori_loop(1, NZ, start_z, 0)
    z_copy(0, 1).start()

    for k in (2, 3):
        block_copy(k, 2).start()

    loads[3].wait()
    loads[6].wait()
    for kind in (0, 1):
        all_blocks(kind).wait_recv()
    for shard in range(NZH * NC):
        rows = pool_tail[shard].astype(jnp.float32)
        for j in range(8):
            tails[shard * 8 + j] = jnp.concatenate([rows[4 * j : 4 * j + 4]] * 4, axis=0)

    def first_channels(t, carry):
        def rows(b):
            last = tails[slot_ref[t, b]].astype(jnp.bfloat16)
            return jnp.concatenate([pool_a[slot_ref[t, b]], last], axis=0)

        left = jnp.concatenate([rows(b) for b in range(8)], axis=1)
        right = weights[t].reshape(-1, weights.shape[-1])
        value = jnp.dot(left, right, preferred_element_type=jnp.float32)
        nodes[pl.ds(t, FIRST, stride=8)] = value[:FIRST]
        nodes[pl.ds(MAIN * 8 + t, 4, stride=8)] = value[FIRST : FIRST + 4]
        return carry

    lax.fori_loop(0, 8, first_channels, 0, unroll=True)
    hidden_ref[: FIRST * 8] = nodes[: FIRST * 8].astype(jnp.bfloat16)
    hidden_ref[MAIN * 8 :] = nodes[MAIN * 8 :].astype(jnp.bfloat16)

    all_z.wait_recv()
    for core in range(NC):
        value = from_z[core]
        for dz in range(1, NZ):
            value = value + from_z[dz * NC + core]
        grad_ref[:, core * half : (core + 1) * half] = value

    all_blocks(2).wait_recv()

    def other_channels(t, carry):
        left = jnp.concatenate([pool_b[slot_ref[t, b]] for b in range(8)], axis=1)
        right = weights[t].reshape(-1, weights.shape[-1])
        nodes[pl.ds(FIRST * 8 + t, MAIN - FIRST, stride=8)] = jnp.dot(
            left, right, preferred_element_type=jnp.float32
        )
        return carry

    lax.fori_loop(0, 8, other_channels, 0, unroll=True)
    hidden_ref[FIRST * 8 : MAIN * 8] = nodes[FIRST * 8 : MAIN * 8].astype(jnp.bfloat16)

    for kind in range(3):
        all_blocks(kind).wait_send()
    all_of(given, d_send.at[0], d_recv.at[0]).wait_send()
    for copies in (all_x, all_y, all_u, all_v, all_z):
        copies.wait_send()


def body(field, send_blocks, send_count, regrid_weights, tile_slot, edge_inputs, cotangent):
    tiles, reads, cells, nodes = regrid_weights.shape
    blocks, channels = field.shape[1:3]
    half = cotangent.shape[1] // 2
    field = jnp.transpose(field, (0, 2, 1, 3)).reshape(channels * blocks, cells)
    f32, bf16 = jnp.float32, jnp.bfloat16
    dma = pltpu.SemaphoreType.DMA
    vmem = pl.BlockSpec(memory_space=pltpu.VMEM)
    hbm = pl.BlockSpec(memory_space=pl.ANY)
    hidden, grad = pl.pallas_call(
        kernel,
        name="regrid",
        out_shape=(
            pltpu.VMEM((channels * tiles, nodes), bf16),
            pltpu.VMEM((2, 2 * half), f32),
        ),
        in_specs=[hbm] * 7,
        out_specs=(vmem, vmem),
        scratch_shapes=[
            pltpu.SMEM(send_blocks.shape, jnp.int32),
            pltpu.SMEM(send_count.shape, jnp.int32),
            pltpu.SMEM(tile_slot.shape, jnp.int32),
            pltpu.VMEM(field.shape, bf16),
            pltpu.VMEM((channels * PITCH, cells), f32),
            pltpu.VMEM(regrid_weights.shape, bf16),
            pltpu.VMEM(edge_inputs.shape, bf16),
            pltpu.VMEM(cotangent.shape, bf16),
            pltpu.VMEM((4, 8, FIRST, cells), bf16),
            pltpu.VMEM((4, 8, MAIN - FIRST, cells), bf16),
            pltpu.VMEM((4, 32, cells), bf16),
            pltpu.VMEM((32, FIRST, cells), bf16),
            pltpu.VMEM((32, MAIN - FIRST, cells), bf16),
            pltpu.VMEM((4, 32, cells), bf16),
            pltpu.VMEM((32, 16, cells), f32),
            pltpu.VMEM((channels * tiles, nodes), f32),
            pltpu.VMEM((2, NY, NX, ROWS, LANES), f32),
            pltpu.VMEM((NY, NX, ROWS, LANES), f32),
            pltpu.VMEM((NY, NX, ROWS, LANES), f32),
            pltpu.VMEM((NY, NX - 1, XROWS, LANES), f32),
            pltpu.VMEM((NY, XROWS, LANES), f32),
            pltpu.VMEM((NY, XROWS, LANES), f32),
            pltpu.VMEM((NY, NX, ROWS - XROWS, LANES), f32),
            pltpu.VMEM((NX, ROWS - XROWS, LANES), f32),
            pltpu.VMEM((NX - 1, ROWS - XROWS, LANES), f32),
            pltpu.VMEM((ROWS, LANES), f32),
            pltpu.VMEM((NZ * NC, 2, half), f32),
            pltpu.VMEM((NZ * NC, 2, half), f32),
            dma((7,)),
            dma((3,)), dma((3,)),
            dma((1,)), dma((NY,)),
            dma((1,)), dma((NY,)),
            dma((1,)), dma((1,)),
            dma((1,)), dma((1,)),
            dma((1,)), dma((1,)),
            dma((1,)), dma((1,)),
        ],
        compiler_params=pltpu.CompilerParams(
            collective_id=0, has_side_effects=True, vmem_limit_bytes=56 * 2**20
        ),
    )(send_blocks, send_count, tile_slot, field, regrid_weights, edge_inputs, cotangent)
    return jnp.transpose(hidden.reshape(1, channels, tiles, nodes), (0, 2, 1, 3)), grad


def solution(mesh):
    split = Mesh(mesh.devices.reshape(NY, NX, NZL, NZH, NC), AXES)
    rep, sp = AXES[:3], AXES[3:]
    return jax.shard_map(
        body,
        mesh=split,
        in_specs=(
            P(rep, sp, None, None),
            P(sp, None, None),
            P(sp, None),
            P(sp, None, None, None),
            P(sp, None),
            P(AXES, None),
            P(AXES, None),
        ),
        out_specs=(P(rep, sp, None, None), P(AXES, None)),
        check_vma=False,
    )
```

time: 61.6 us -> 52.6 us (0.85)
  Pallas kernels: 55.4 us -> 50.5 us
  local copies, waits for them, and re-layouts: 5.28 us -> 1.27 us
    pallas_call x1, Pallas kernels: 55.4 us -> 50.5 us  [body(): pl.pallas_call(kernel, name='regrid', out_shape=(pltpu.VMEM((channels * t...]
    unnamed x2, local copies, waits for them, and re-layouts: 3.63 us -> 1.27 us
    pallas_call x1 -> x0, local copies, waits for them, and re-layouts: 1.64 us -> none  [body(): pl.pallas_call(kernel, name='regrid', out_shape=(jax.ShapeDtypeStruct((1,...]
where the time goes in v2:
time: 52.6 us; the launch traced here: 52.4 us
  Pallas kernels  50.5 us (96%)
  local copies, waits for them, and re-layouts  1.27 us (2%)
  between operations  0.64 us (1%)
    pallas_call x1, Pallas kernels, body(): pl.pallas_call(kernel, name='regrid', out_shape=(pltpu.VMEM((channels * t...  50.5 us
    unnamed x2, local copies, waits for them, and re-layouts  1.27 us

profile of v2, /device:TPU:1, one launch (start us, length us, event | category | flops | bytes accessed | tf_op | source)
XLA Modules:
  0.0 52.4 jit_solution(9913321684408368719)
XLA Ops:
  0.6 50.5 %regrid.1 = (bf16[800,128]{1,0:T(8,128)(2,1)S(1)}, f32[2,512]{1,0:T(2,128)S(1)}) custom-call(s32[1,4,8]{2,1,0:T(4,128)} %blocks_hbm.1, s32[1,4]{1,0:T(1,128)} %count_hbm.1, s32[8,8]{1,0:T(8,128)} %slot_hbm.1, bf16[3200,128]{1,0:T(8,128)(2,1)} %bitcast.7, bf16[8,8,128,128]{3,2,1,0:T(8,128)(2,1)} %weights_hbm.1, bf16[384,1536]{1,0:T(8,128)(2,1)} %edges_hbm.1, ...), custom_call_target="tpu_custom_call" | custom-call | tf_op jit(solution)/shard_map/regrid/pallas_call | solution.py:334
  51.2 0.7 %copy.11 = bf16[1,8,100,128]{3,1,2,0:T(8,128)(2,1)} copy(bf16[1,8,100,128]{3,1,2,0:T(8,128)(2,1)S(1)} %bitcast.6) | data formatting | bytes 409600
  51.8 0.6 %copy.12 = f32[2,512]{1,0:T(2,128)} copy(f32[2,512]{1,0:T(2,128)S(1)} %get-tuple-element.7) | data formatting | bytes 8192

commit v3 on v2

--- a/solution.py
+++ b/solution.py
@@ -11,7 +11,8 @@
 NZ = NZL * NZH
 LANES = 128
 ROWS = 96
-FIRST = 80
+FIRST = 64
+LATER = 16
 MAIN = 96
 PITCH = 40
 XROWS = 72
@@ -22,9 +23,9 @@
     blocks_hbm, count_hbm, slot_hbm, field_hbm, weights_hbm, edges_hbm, cot_hbm,
     hidden_ref, grad_ref,
     blocks_ref, count_ref, slot_ref, field, wide, weights, edges, cot,
-    out_a, out_b, out_tail, pool_a, pool_b, pool_tail, tails, nodes,
+    out_a, out_b, out_tail, pool_a, pool_b, pool_c, pool_tail, tails, nodes,
     part, given, chip, from_x, sum_x, from_y, last_y, sum_y, last_x, total, to_z, from_z,
-    in_sem, a_send, a_recv, d_send, d_recv, x_send, x_recv, y_send, y_recv,
+    near, far, in_sem, a_send, a_recv, d_send, d_recv, x_send, x_recv, y_send, y_recv,
     u_send, u_recv, v_send, v_recv, z_send, z_recv,
 ):
     y, x = lax.axis_index("y"), lax.axis_index("x")
@@ -55,15 +56,16 @@
     def greet(**offset):
         pl.semaphore_signal(barrier, inc=1, device_id=at(**offset), device_id_type=MESH)
 
-    for k in (6, 5, 7, 4, 8, 3, 9, 2, 10, 1, 11):
+    greet(dz=NZL)
+    greet(dz=NZL, dc=1)
+    for load in loads:
+        load.start()
+    for k in (1, NZ - 1):
         greet(dz=k)
         greet(dz=k, dc=1)
-        if k == 6:
-            for load in loads:
-                load.start()
-    for k in (4, 3, 5, 2, 6, 1, 7):
+    for k in (1, NY - 1):
         greet(dy=k)
-    for k in (2, 1, 3):
+    for k in (1, NX - 1):
         greet(dx=k)
     greet(dc=1)
 
@@ -90,7 +92,8 @@
             main = wide[pl.ds(start, MAIN, stride=PITCH)]
             main = jnp.where(alive, main, jnp.zeros_like(main)).astype(jnp.bfloat16)
             out_a[k, j] = main[:FIRST]
-            out_b[k, j] = main[FIRST:]
+            out_b[0, k, j] = main[FIRST : FIRST + LATER]
+            out_b[1, k, j] = main[FIRST + LATER :]
             tail = wide[pl.ds(start + MAIN * PITCH, 4, stride=PITCH)]
             last.append(jnp.where(alive, tail, jnp.zeros_like(tail)))
         out_tail[k] = jnp.concatenate(last, axis=0).astype(jnp.bfloat16)
@@ -98,24 +101,41 @@
 
     lax.fori_loop(0, 4, gather, 0)
     pool_a[pl.ds(own * 8, 8)] = out_a[0]
-    pool_b[pl.ds(own * 8, 8)] = out_b[0]
+    for later in range(2):
+        (pool_b, pool_c)[later][pl.ds(own * 8, 8)] = out_b[later, 0]
     pool_tail[own] = out_tail[0]
 
-    loads[1].wait()
-    loads[2].wait()
-    for k in range(4):
-        piece = lax.dot_general(
-            edges[:, k * 384 : (k + 1) * 384], cot[...], (((0,), (0,)), ((), ())),
-            preferred_element_type=jnp.float32,
-        )
-        for h in range(2):
-            for g in range(2):
-                column = h * half + g * LANES
-                part[h, 2 * k : 2 * k + 2, :, g * 48 : g * 48 + 48] = piece[:, column : column + LANES].reshape(
-                    2, NX, 48, LANES
-                )
-
-    pl.semaphore_wait(barrier, 2 * (NZ - 1) + (NY - 1) + (NX - 1) + 1)
+    def own_gradient():
+        loads[1].wait()
+        loads[2].wait()
+        for k in range(4):
+            piece = lax.dot_general(
+                edges[:, k * 384 : (k + 1) * 384], cot[...], (((0,), (0,)), ((), ())),
+                preferred_element_type=jnp.float32,
+            )
+            for h in range(2):
+                for g in range(2):
+                    column = h * half + g * LANES
+                    part[h, 2 * k : 2 * k + 2, :, g * 48 : g * 48 + 48] = piece[:, column : column + LANES].reshape(
+                        2, NX, 48, LANES
+                    )
+
+    @pl.when(zh == 0)
+    def _():
+        own_gradient()
+
+    pl.semaphore_wait(barrier, 11)
+
+    def tell_xy(r):
+        first = (dict(dy=1), dict(dy=NY - 1), dict(dx=1), dict(dx=NX - 1))
+        second = (dict(dy=1), dict(dy=NY - 1), dict(dy=2), dict(dy=NY - 2))
+        for offset in (first, second)[r]:
+            pl.semaphore_signal(near.at[r], inc=1, device_id=at(**offset), device_id_type=MESH)
+
+    def tell_z(r):
+        for k in (NZL, 1, NZ - 1):
+            pl.semaphore_signal(far.at[r], inc=1, device_id=at(dz=k), device_id_type=MESH)
+
 
     def remote(source, goal, send, recv, **offset):
         return pltpu.make_async_remote_copy(
@@ -127,19 +147,35 @@
         source, goal = (
             (out_a.at[k], pool_a.at[pl.ds(own * 8, 8)]),
             (out_tail.at[k], pool_tail.at[own]),
-            (out_b.at[k], pool_b.at[pl.ds(own * 8, 8)]),
+            (out_b.at[0, k], pool_b.at[pl.ds(own * 8, 8)]),
+            (out_b.at[1, k], pool_c.at[pl.ds(own * 8, 8)]),
         )[kind]
         return remote(source, goal, a_send.at[kind], a_recv.at[kind], dz=NZL * (k // 2), dc=k % 2)
 
     def all_blocks(kind):
-        whole = (pool_a.at[pl.ds(0, 24)], pool_tail.at[pl.ds(0, 3)], pool_b.at[pl.ds(0, 24)])[kind]
+        whole = (
+            pool_a.at[pl.ds(0, 24)], pool_tail.at[pl.ds(0, 3)],
+            pool_b.at[pl.ds(0, 24)], pool_c.at[pl.ds(0, 24)],
+        )[kind]
         return remote(whole, whole, a_send.at[kind], a_recv.at[kind], dc=1)
 
     for k in (2, 3):
         for kind in (0, 1):
             block_copy(k, kind).start()
-    for kind in range(3):
+
+    @pl.when(zh == 1)
+    def _():
+        for k in (2, 3):
+            block_copy(k, 2).start()
+
+    for kind in range(4):
         block_copy(1, kind).start()
+
+    tell_xy(0)
+
+    @pl.when(zh == 1)
+    def _():
+        own_gradient()
 
     def away(k):
         return 4 + lax.div(k, 2) * (1 - 2 * lax.rem(k, 2)) - lax.rem(k, 2)
@@ -179,24 +215,39 @@
         return carry
 
     lax.fori_loop(0, NY, start_core, 0)
+    tell_z(0)
 
     def send_x(k):
         dy = away(k)
         for dx in (2, 1, 3):
             x_copy(dx, dy).start()
 
-        @pl.when(dy > 0)
-        def _():
-            u_copy(dy).start()
-
     def over_cores(k, carry):
         dy = away(k)
         core_copy(dy).wait_recv()
         chip[dy] = part[c, lax.rem(y + dy, NY)] + given[dy]
 
+        @pl.when(k == 0)
+        def _():
+            pl.semaphore_wait(near.at[0], 4)
+            tell_xy(1)
+
         @pl.when(k > 0)
         def _():
             send_x(k - 1)
+
+        @pl.when(k == 2)
+        def _():
+            pl.semaphore_wait(near.at[1], 4)
+
+        @pl.when((k == 3) | (k == 4))
+        def _():
+            u_copy(away(2 * k - 6)).start()
+            u_copy(away(2 * k - 5)).start()
+
+        @pl.when(k > 4)
+        def _():
+            u_copy(away(k - 1)).start()
 
         return carry
 
@@ -218,6 +269,11 @@
         @pl.when(k > 0)
         def _():
             send_y(k - 1)
+
+        @pl.when(k == 3)
+        def _():
+            pl.semaphore_wait(far.at[0], 3)
+            tell_z(1)
 
         return carry
 
@@ -259,6 +315,8 @@
     all_z = all_of(from_z.at[pl.ds(0, NZ * NC - 1)], z_send.at[0], z_recv.at[0])
     from_z[c] = to_z[z * NC + c]
 
+    pl.semaphore_wait(far.at[1], 3)
+
     def start_z(k, carry):
         z_copy(k, 0).start()
         z_copy(k, 1).start()
@@ -267,8 +325,13 @@
     lax.fori_loop(1, NZ, start_z, 0)
     z_copy(0, 1).start()
 
+    @pl.when(zh == 0)
+    def _():
+        for k in (2, 3):
+            block_copy(k, 2).start()
+
     for k in (2, 3):
-        block_copy(k, 2).start()
+        block_copy(k, 3).start()
 
     loads[3].wait()
     loads[6].wait()
@@ -295,6 +358,19 @@
     hidden_ref[: FIRST * 8] = nodes[: FIRST * 8].astype(jnp.bfloat16)
     hidden_ref[MAIN * 8 :] = nodes[MAIN * 8 :].astype(jnp.bfloat16)
 
+    def other_channels(p):
+        all_blocks(2 + p).wait_recv()
+        start = FIRST + p * LATER
+        pool = (pool_b, pool_c)[p]
+        for t in range(8):
+            left = jnp.concatenate([pool[slot_ref[t, b]] for b in range(8)], axis=1)
+            right = weights[t].reshape(-1, weights.shape[-1])
+            nodes[pl.ds(start * 8 + t, LATER, stride=8)] = jnp.dot(left, right, preferred_element_type=jnp.float32)
+        rows = slice(start * 8, (start + LATER) * 8)
+        hidden_ref[rows] = nodes[rows].astype(jnp.bfloat16)
+
+    other_channels(0)
+
     all_z.wait_recv()
     for core in range(NC):
         value = from_z[core]
@@ -302,20 +378,9 @@
             value = value + from_z[dz * NC + core]
         grad_ref[:, core * half : (core + 1) * half] = value
 
-    all_blocks(2).wait_recv()
-
-    def other_channels(t, carry):
-        left = jnp.concatenate([pool_b[slot_ref[t, b]] for b in range(8)], axis=1)
-        right = weights[t].reshape(-1, weights.shape[-1])
-        nodes[pl.ds(FIRST * 8 + t, MAIN - FIRST, stride=8)] = jnp.dot(
-            left, right, preferred_element_type=jnp.float32
-        )
-        return carry
-
-    lax.fori_loop(0, 8, other_channels, 0, unroll=True)
-    hidden_ref[FIRST * 8 : MAIN * 8] = nodes[FIRST * 8 : MAIN * 8].astype(jnp.bfloat16)
-
-    for kind in range(3):
+    other_channels(1)
+
+    for kind in range(4):
         all_blocks(kind).wait_send()
     all_of(given, d_send.at[0], d_recv.at[0]).wait_send()
     for copies in (all_x, all_y, all_u, all_v, all_z):
@@ -350,10 +415,11 @@
             pltpu.VMEM(edge_inputs.shape, bf16),
             pltpu.VMEM(cotangent.shape, bf16),
             pltpu.VMEM((4, 8, FIRST, cells), bf16),
-            pltpu.VMEM((4, 8, MAIN - FIRST, cells), bf16),
+            pltpu.VMEM((2, 4, 8, LATER, cells), bf16),
             pltpu.VMEM((4, 32, cells), bf16),
             pltpu.VMEM((32, FIRST, cells), bf16),
-            pltpu.VMEM((32, MAIN - FIRST, cells), bf16),
+            pltpu.VMEM((32, LATER, cells), bf16),
+            pltpu.VMEM((32, LATER, cells), bf16),
             pltpu.VMEM((4, 32, cells), bf16),
             pltpu.VMEM((32, 16, cells), f32),
             pltpu.VMEM((channels * tiles, nodes), f32),
@@ -369,8 +435,10 @@
             pltpu.VMEM((ROWS, LANES), f32),
             pltpu.VMEM((NZ * NC, 2, half), f32),
             pltpu.VMEM((NZ * NC, 2, half), f32),
+            pltpu.SemaphoreType.REGULAR((2,)),
+            pltpu.SemaphoreType.REGULAR((2,)),
             dma((7,)),
-            dma((3,)), dma((3,)),
+            dma((4,)), dma((4,)),
             dma((1,)), dma((NY,)),
             dma((1,)), dma((NY,)),
             dma((1,)), dma((1,)),

time: 52.6 us -> 51.7 us (0.983)
  the two profiles are of different devices: /device:TPU:1 before, /device:TPU:13 now
where the time goes in v3:
time: 51.7 us; the launch traced here: 51.6 us
  Pallas kernels  49.7 us (96%)
  local copies, waits for them, and re-layouts  1.27 us (2%)
  between operations  0.64 us (1%)
    pallas_call x1, Pallas kernels, body(): pl.pallas_call(kernel, name='regrid', out_shape=(pltpu.VMEM((channels * t...  49.7 us
    unnamed x2, local copies, waits for them, and re-layouts  1.27 us

profile of v3, /device:TPU:13, one launch (start us, length us, event | category | flops | bytes accessed | tf_op | source)
XLA Modules:
  0.0 51.6 jit_solution(7820074835678365286)
XLA Ops:
  0.6 49.7 %regrid.1 = (bf16[800,128]{1,0:T(8,128)(2,1)S(1)}, f32[2,512]{1,0:T(2,128)S(1)}) custom-call(s32[1,4,8]{2,1,0:T(4,128)} %blocks_hbm.1, s32[1,4]{1,0:T(1,128)} %count_hbm.1, s32[8,8]{1,0:T(8,128)} %slot_hbm.1, bf16[3200,128]{1,0:T(8,128)(2,1)} %bitcast.7, bf16[8,8,128,128]{3,2,1,0:T(8,128)(2,1)} %weights_hbm.1, bf16[384,1536]{1,0:T(8,128)(2,1)} %edges_hbm.1, ...), custom_call_target="tpu_custom_call" | custom-call | tf_op jit(solution)/shard_map/regrid/pallas_call | solution.py:399
  50.3 0.7 %copy.11 = bf16[1,8,100,128]{3,1,2,0:T(8,128)(2,1)} copy(bf16[1,8,100,128]{3,1,2,0:T(8,128)(2,1)S(1)} %bitcast.6) | data formatting | bytes 409600
  51.0 0.6 %copy.12 = f32[2,512]{1,0:T(2,128)} copy(f32[2,512]{1,0:T(2,128)S(1)} %get-tuple-element.7) | data formatting | bytes 8192

commit v4 on v3

--- a/solution.py
+++ b/solution.py
@@ -11,9 +11,8 @@
 NZ = NZL * NZH
 LANES = 128
 ROWS = 96
-FIRST = 64
-LATER = 16
-MAIN = 96
+FIRST, SECOND, THIRD = 64, 16, 16
+MAIN = FIRST + SECOND + THIRD
 PITCH = 40
 XROWS = 72
 MESH = pl.DeviceIdType.MESH
@@ -23,8 +22,8 @@
     blocks_hbm, count_hbm, slot_hbm, field_hbm, weights_hbm, edges_hbm, cot_hbm,
     hidden_ref, grad_ref,
     blocks_ref, count_ref, slot_ref, field, wide, weights, edges, cot,
-    out_a, out_b, out_tail, pool_a, pool_b, pool_c, pool_tail, tails, nodes,
-    part, given, chip, from_x, sum_x, from_y, last_y, sum_y, last_x, total, to_z, from_z,
+    out_a, out_b, out_c, out_tail, pool_a, pool_b, pool_c, pool_tail, tails, nodes,
+    part, given, chip, from_x, sum_x, from_y, last_y, sum_y, last_x, total, to_z, from_z, to_core, from_core,
     near, far, in_sem, a_send, a_recv, d_send, d_recv, x_send, x_recv, y_send, y_recv,
     u_send, u_recv, v_send, v_recv, z_send, z_recv,
 ):
@@ -92,8 +91,8 @@
             main = wide[pl.ds(start, MAIN, stride=PITCH)]
             main = jnp.where(alive, main, jnp.zeros_like(main)).astype(jnp.bfloat16)
             out_a[k, j] = main[:FIRST]
-            out_b[0, k, j] = main[FIRST : FIRST + LATER]
-            out_b[1, k, j] = main[FIRST + LATER :]
+            out_b[k, j] = main[FIRST : FIRST + SECOND]
+            out_c[k, j] = main[FIRST + SECOND :]
             tail = wide[pl.ds(start + MAIN * PITCH, 4, stride=PITCH)]
             last.append(jnp.where(alive, tail, jnp.zeros_like(tail)))
         out_tail[k] = jnp.concatenate(last, axis=0).astype(jnp.bfloat16)
@@ -101,8 +100,8 @@
 
     lax.fori_loop(0, 4, gather, 0)
     pool_a[pl.ds(own * 8, 8)] = out_a[0]
-    for later in range(2):
-        (pool_b, pool_c)[later][pl.ds(own * 8, 8)] = out_b[later, 0]
+    pool_b[pl.ds(own * 8, 8)] = out_b[0]
+    pool_c[pl.ds(own * 8, 8)] = out_c[0]
     pool_tail[own] = out_tail[0]
 
     def own_gradient():
@@ -147,8 +146,8 @@
         source, goal = (
             (out_a.at[k], pool_a.at[pl.ds(own * 8, 8)]),
             (out_tail.at[k], pool_tail.at[own]),
-            (out_b.at[0, k], pool_b.at[pl.ds(own * 8, 8)]),
-            (out_b.at[1, k], pool_c.at[pl.ds(own * 8, 8)]),
+            (out_b.at[k], pool_b.at[pl.ds(own * 8, 8)]),
+            (out_c.at[k], pool_c.at[pl.ds(own * 8, 8)]),
         )[kind]
         return remote(source, goal, a_send.at[kind], a_recv.at[kind], dz=NZL * (k // 2), dc=k % 2)
 
@@ -159,14 +158,16 @@
         )[kind]
         return remote(whole, whole, a_send.at[kind], a_recv.at[kind], dc=1)
 
-    for k in (2, 3):
-        for kind in (0, 1):
-            block_copy(k, kind).start()
+    def send_blocks_of(kinds):
+        for k in (2, 3):
+            for kind in kinds:
+                block_copy(k, kind).start()
+
+    send_blocks_of((0, 1))
 
     @pl.when(zh == 1)
     def _():
-        for k in (2, 3):
-            block_copy(k, 2).start()
+        send_blocks_of((2,))
 
     for kind in range(4):
         block_copy(1, kind).start()
@@ -302,36 +303,33 @@
         for group in range(2):
             tile = total[group * 48 + low * 8 : group * 48 + low * 8 + 8]
             for high in range(NZH):
-                for core in range(NC):
-                    row = high * 4 + core * 2
-                    to_z[(high * NZL + low) * NC + core, :, group * LANES : (group + 1) * LANES] = tile[row : row + 2]
-
-    def z_copy(dz, dc):
-        return remote(
-            to_z.at[lax.rem(z + dz, NZ) * NC + lax.rem(c + dc, NC)], from_z.at[dz * NC + c],
-            z_send.at[0], z_recv.at[0], dz=dz, dc=dc,
-        )
-
-    all_z = all_of(from_z.at[pl.ds(0, NZ * NC - 1)], z_send.at[0], z_recv.at[0])
-    from_z[c] = to_z[z * NC + c]
+                to_z[high * NZL + low, :, group * LANES : (group + 1) * LANES] = tile[high * 4 : high * 4 + 4]
+
+    def z_copy(target):
+        dz = lax.rem(target - z + NZ, NZ)
+        return remote(to_z.at[target], from_z.at[dz], z_send.at[0], z_recv.at[0], dz=dz)
+
+    all_z = all_of(from_z.at[pl.ds(1, NZ - 1)], z_send.at[0], z_recv.at[0])
+    from_z[0] = to_z[z]
 
     pl.semaphore_wait(far.at[1], 3)
 
-    def start_z(k, carry):
-        z_copy(k, 0).start()
-        z_copy(k, 1).start()
-        return carry
-
-    lax.fori_loop(1, NZ, start_z, 0)
-    z_copy(0, 1).start()
+    def start_z(target, carry):
+        @pl.when(target != z)
+        def _():
+            z_copy(target).start()
+
+        return carry
+
+    lax.fori_loop(0, NZ, start_z, 0)
 
     @pl.when(zh == 0)
     def _():
-        for k in (2, 3):
-            block_copy(k, 2).start()
-
-    for k in (2, 3):
-        block_copy(k, 3).start()
+        send_blocks_of((2, 3))
+
+    @pl.when(zh == 1)
+    def _():
+        send_blocks_of((3,))
 
     loads[3].wait()
     loads[6].wait()
@@ -360,30 +358,36 @@
 
     def other_channels(p):
         all_blocks(2 + p).wait_recv()
-        start = FIRST + p * LATER
-        pool = (pool_b, pool_c)[p]
+        start, size, pool = ((FIRST, SECOND, pool_b), (FIRST + SECOND, THIRD, pool_c))[p]
         for t in range(8):
             left = jnp.concatenate([pool[slot_ref[t, b]] for b in range(8)], axis=1)
             right = weights[t].reshape(-1, weights.shape[-1])
-            nodes[pl.ds(start * 8 + t, LATER, stride=8)] = jnp.dot(left, right, preferred_element_type=jnp.float32)
-        rows = slice(start * 8, (start + LATER) * 8)
+            nodes[pl.ds(start * 8 + t, size, stride=8)] = jnp.dot(left, right, preferred_element_type=jnp.float32)
+        rows = slice(start * 8, (start + size) * 8)
         hidden_ref[rows] = nodes[rows].astype(jnp.bfloat16)
 
     other_channels(0)
 
     all_z.wait_recv()
+    value = from_z[0]
+    for dz in range(1, NZ):
+        value = value + from_z[dz]
     for core in range(NC):
-        value = from_z[core]
-        for dz in range(1, NZ):
-            value = value + from_z[dz * NC + core]
-        grad_ref[:, core * half : (core + 1) * half] = value
-
+        to_core[core] = value[2 * core : 2 * core + 2]
+
+    last_copy = remote(to_core.at[1 - c], from_core, d_send.at[1], d_recv.at[NY], dc=1)
+    last_copy.start()
     other_channels(1)
+
+    last_copy.wait_recv()
+    mine, other = to_core[c], from_core[...]
+    grad_ref[:, :half] = jnp.where(c == 0, mine, other)
+    grad_ref[:, half:] = jnp.where(c == 0, other, mine)
 
     for kind in range(4):
         all_blocks(kind).wait_send()
     all_of(given, d_send.at[0], d_recv.at[0]).wait_send()
-    for copies in (all_x, all_y, all_u, all_v, all_z):
+    for copies in (all_x, all_y, all_u, all_v, all_z, last_copy):
         copies.wait_send()
 
 
@@ -415,11 +419,12 @@
             pltpu.VMEM(edge_inputs.shape, bf16),
             pltpu.VMEM(cotangent.shape, bf16),
             pltpu.VMEM((4, 8, FIRST, cells), bf16),
-            pltpu.VMEM((2, 4, 8, LATER, cells), bf16),
+            pltpu.VMEM((4, 8, SECOND, cells), bf16),
+            pltpu.VMEM((4, 8, THIRD, cells), bf16),
             pltpu.VMEM((4, 32, cells), bf16),
             pltpu.VMEM((32, FIRST, cells), bf16),
-            pltpu.VMEM((32, LATER, cells), bf16),
-            pltpu.VMEM((32, LATER, cells), bf16),
+            pltpu.VMEM((32, SECOND, cells), bf16),
+            pltpu.VMEM((32, THIRD, cells), bf16),
             pltpu.VMEM((4, 32, cells), bf16),
             pltpu.VMEM((32, 16, cells), f32),
             pltpu.VMEM((channels * tiles, nodes), f32),
@@ -433,13 +438,15 @@
             pltpu.VMEM((NX, ROWS - XROWS, LANES), f32),
             pltpu.VMEM((NX - 1, ROWS - XROWS, LANES), f32),
             pltpu.VMEM((ROWS, LANES), f32),
-            pltpu.VMEM((NZ * NC, 2, half), f32),
-            pltpu.VMEM((NZ * NC, 2, half), f32),
+            pltpu.VMEM((NZ, 4, half), f32),
+            pltpu.VMEM((NZ, 4, half), f32),
+            pltpu.VMEM((NC, 2, half), f32),
+            pltpu.VMEM((2, half), f32),
             pltpu.SemaphoreType.REGULAR((2,)),
             pltpu.SemaphoreType.REGULAR((2,)),
             dma((7,)),
             dma((4,)), dma((4,)),
-            dma((1,)), dma((NY,)),
+            dma((2,)), dma((NY + 1,)),
             dma((1,)), dma((NY,)),
             dma((1,)), dma((1,)),
             dma((1,)), dma((1,)),

time: 51.7 us -> 50 us (0.967)
  the two profiles are of different devices: /device:TPU:13 before, /device:TPU:1 now
where the time goes in v4:
time: 50 us; the launch traced here: 49.9 us
  Pallas kernels  47.9 us (96%)
  local copies, waits for them, and re-layouts  1.27 us (3%)
  between operations  0.64 us (1%)
    pallas_call x1, Pallas kernels, body(): pl.pallas_call(kernel, name='regrid', out_shape=(pltpu.VMEM((channels * t...  47.9 us
    unnamed x2, local copies, waits for them, and re-layouts  1.27 us

profile of v4, /device:TPU:1, one launch (start us, length us, event | category | flops | bytes accessed | tf_op | source)
XLA Modules:
  0.0 49.9 jit_solution(17866025270133022834)
XLA Ops:
  0.6 47.9 %regrid.1 = (bf16[800,128]{1,0:T(8,128)(2,1)S(1)}, f32[2,512]{1,0:T(2,128)S(1)}) custom-call(s32[1,4,8]{2,1,0:T(4,128)} %blocks_hbm.1, s32[1,4]{1,0:T(1,128)} %count_hbm.1, s32[8,8]{1,0:T(8,128)} %slot_hbm.1, bf16[3200,128]{1,0:T(8,128)(2,1)} %bitcast.7, bf16[8,8,128,128]{3,2,1,0:T(8,128)(2,1)} %weights_hbm.1, bf16[384,1536]{1,0:T(8,128)(2,1)} %edges_hbm.1, ...), custom_call_target="tpu_custom_call" | custom-call | tf_op jit(solution)/shard_map/regrid/pallas_call | solution.py:403
  48.6 0.7 %copy.11 = bf16[1,8,100,128]{3,1,2,0:T(8,128)(2,1)} copy(bf16[1,8,100,128]{3,1,2,0:T(8,128)(2,1)S(1)} %bitcast.6) | data formatting | bytes 409600
  49.3 0.6 %copy.12 = f32[2,512]{1,0:T(2,128)} copy(f32[2,512]{1,0:T(2,128)S(1)} %get-tuple-element.7) | data formatting | bytes 8192

commit v5 on v4

--- a/solution.py
+++ b/solution.py
@@ -14,7 +14,7 @@
 FIRST, SECOND, THIRD = 64, 16, 16
 MAIN = FIRST + SECOND + THIRD
 PITCH = 40
-XROWS = 72
+XROWS = 80
 MESH = pl.DeviceIdType.MESH
 
 
@@ -321,15 +321,17 @@
 
         return carry
 
-    lax.fori_loop(0, NZ, start_z, 0)
+    lax.fori_loop(0, NZL, start_z, 0)
+
+    @pl.when(zh == 1)
+    def _():
+        send_blocks_of((3,))
+
+    lax.fori_loop(NZL, NZ, start_z, 0)
 
     @pl.when(zh == 0)
     def _():
         send_blocks_of((2, 3))
-
-    @pl.when(zh == 1)
-    def _():
-        send_blocks_of((3,))
 
     loads[3].wait()
     loads[6].wait()

time: 50 us -> 49.9 us (level)
  no operation moved by 1% of the time
where the time goes in v5:
time: 49.9 us; the launch traced here: 49.7 us
  Pallas kernels  47.8 us (96%)
  local copies, waits for them, and re-layouts  1.27 us (3%)
  between operations  0.64 us (1%)
    pallas_call x1, Pallas kernels, body(): pl.pallas_call(kernel, name='regrid', out_shape=(pltpu.VMEM((channels * t...  47.8 us
    unnamed x2, local copies, waits for them, and re-layouts  1.27 us

profile of v5, /device:TPU:1, one launch (start us, length us, event | category | flops | bytes accessed | tf_op | source)
XLA Modules:
  0.0 49.7 jit_solution(2585075275862211026)
XLA Ops:
  0.6 47.8 %regrid.1 = (bf16[800,128]{1,0:T(8,128)(2,1)S(1)}, f32[2,512]{1,0:T(2,128)S(1)}) custom-call(s32[1,4,8]{2,1,0:T(4,128)} %blocks_hbm.1, s32[1,4]{1,0:T(1,128)} %count_hbm.1, s32[8,8]{1,0:T(8,128)} %slot_hbm.1, bf16[3200,128]{1,0:T(8,128)(2,1)} %bitcast.7, bf16[8,8,128,128]{3,2,1,0:T(8,128)(2,1)} %weights_hbm.1, bf16[384,1536]{1,0:T(8,128)(2,1)} %edges_hbm.1, ...), custom_call_target="tpu_custom_call" | custom-call | tf_op jit(solution)/shard_map/regrid/pallas_call | solution.py:405
  48.5 0.7 %copy.11 = bf16[1,8,100,128]{3,1,2,0:T(8,128)(2,1)} copy(bf16[1,8,100,128]{3,1,2,0:T(8,128)(2,1)S(1)} %bitcast.6) | data formatting | bytes 409600
  49.1 0.6 %copy.12 = f32[2,512]{1,0:T(2,128)} copy(f32[2,512]{1,0:T(2,128)S(1)} %get-tuple-element.7) | data formatting | bytes 8192

commit v6 on v4

--- a/solution.py
+++ b/solution.py
@@ -389,6 +389,17 @@
     all_of(given, d_send.at[0], d_recv.at[0]).wait_send()
     for copies in (all_x, all_y, all_u, all_v, all_z, last_copy):
         copies.wait_send()
+
+
+def hand_over(hidden_ref, grad_ref, hidden_out, grad_out, sems):
+    copies = [
+        pltpu.make_async_copy(hidden_ref, hidden_out, sems.at[0]),
+        pltpu.make_async_copy(grad_ref, grad_out, sems.at[1]),
+    ]
+    for copy in copies:
+        copy.start()
+    for copy in copies:
+        copy.wait()
 
 
 def body(field, send_blocks, send_count, regrid_weights, tile_slot, edge_inputs, cotangent):
@@ -457,6 +468,20 @@
             collective_id=0, has_side_effects=True, vmem_limit_bytes=56 * 2**20
         ),
     )(send_blocks, send_count, tile_slot, field, regrid_weights, edge_inputs, cotangent)
+    hidden, grad = pl.pallas_call(
+        hand_over,
+        name="hand_over",
+        out_shape=(
+            jax.ShapeDtypeStruct(hidden.shape, bf16),
+            jax.ShapeDtypeStruct(grad.shape, f32),
+        ),
+        in_specs=[pl.BlockSpec(memory_space=pltpu.VMEM)] * 2,
+        out_specs=(hbm, hbm),
+        scratch_shapes=[dma((2,))],
+    )(
+        pltpu.with_memory_space_constraint(hidden, pltpu.VMEM),
+        pltpu.with_memory_space_constraint(grad, pltpu.VMEM),
+    )
     return jnp.transpose(hidden.reshape(1, channels, tiles, nodes), (0, 2, 1, 3)), grad
 
 

time: 50 us -> 49.4 us (0.988)
  local copies, waits for them, and re-layouts: 1.27 us -> 0 us
  Pallas kernels: 47.9 us -> 48.6 us
    unnamed x2 -> x0, local copies, waits for them, and re-layouts: 1.27 us -> none
    pallas_call x0 -> x1, Pallas kernels: none -> 0.7 us  [body(): pl.pallas_call(hand_over, name='hand_over', out_shape=(jax.ShapeDtypeStru...]
where the time goes in v6:
time: 49.4 us; the launch traced here: 49.3 us
  Pallas kernels  48.6 us (98%)
  between operations  0.64 us (1%)
    pallas_call x1, Pallas kernels, body(): pl.pallas_call(kernel, name='regrid', out_shape=(pltpu.VMEM((channels * t...  47.9 us

profile of v6, /device:TPU:1, one launch (start us, length us, event | category | flops | bytes accessed | tf_op | source)
XLA Modules:
  0.0 49.3 jit_solution(8300230978883595692)
XLA Ops:
  0.6 47.9 %regrid.1 = (bf16[800,128]{1,0:T(8,128)(2,1)S(1)}, f32[2,512]{1,0:T(2,128)S(1)}) custom-call(s32[1,4,8]{2,1,0:T(4,128)} %blocks_hbm.1, s32[1,4]{1,0:T(1,128)} %count_hbm.1, s32[8,8]{1,0:T(8,128)} %slot_hbm.1, bf16[3200,128]{1,0:T(8,128)(2,1)} %bitcast.6, bf16[8,8,128,128]{3,2,1,0:T(8,128)(2,1)} %weights_hbm.1, bf16[384,1536]{1,0:T(8,128)(2,1)} %edges_hbm.1, ...), custom_call_target="tpu_custom_call" | custom-call | tf_op jit(solution)/shard_map/regrid/pallas_call | solution.py:414
  48.6 0.7 %hand_over.1 = (bf16[800,128]{1,0:T(8,128)(2,1)}, f32[2,512]{1,0:T(2,128)}) custom-call(bf16[800,128]{1,0:T(8,128)(2,1)S(1)} %get-tuple-element.6.hidden_ref, f32[2,512]{1,0:T(2,128)S(1)} %get-tuple-element.7.grad_ref), custom_call_target="tpu_custom_call" | custom-call | tf_op jit(solution)/shard_map/hand_over/pallas_call | solution.py:471
